TPU v7x, 32 devices: a whole 2x2x4 slice. The times are simulated.
32 devices in a mesh: ex: 8 (over y, x, core), tp: 4 (over z).
Axes of the slice: x: 2, y: 2, z: 4, core: 2. Of those that a mesh axis runs over, the one named last changes fastest.
Arguments:
- samples: bfloat16 [192, 2048], P(('ex', 'tp')), may hold values from -6 to 6
- gate_weight: bfloat16 [2048, 44], replicated, may hold values from -15 to 15
- up_weight: bfloat16 [16, 2048, 4096], P('ex', None, 'tp'), may hold values from -0.125 to 0.125
- down_weight: bfloat16 [16, 4096, 2048], P('ex', 'tp'), may hold values from -0.09375 to 0.09375
Outputs:
- task_outputs: bfloat16 [192, 5, 2048], P(('ex', 'tp'))
All inputs are finite; a program needn't handle non-finite values.
Results may differ from a plain program's by a relative error of at most 0.0055.
Values may be sent and summed in bfloat16 or wider, within the bound.
A program may use at most 128 MiB of HBM per device.

v0:
```python
import jax
import jax.numpy as jnp
import numpy as np
from jax import lax
from jax.sharding import PartitionSpec as P

TASKS = 4
TASK_EXP = 3
SHARED = 4
EXPERTS = 16
GATES = 44


def routing_table():
    per_task = TASK_EXP + SHARED
    table = np.zeros((GATES, (TASKS + 1) * EXPERTS), np.float32)
    for task_idx in range(TASKS):
        for column in range(per_task):
            if column < TASK_EXP:
                expert_idx = task_idx * TASK_EXP + column
            else:
                expert_idx = TASKS * TASK_EXP + column - TASK_EXP
            table[task_idx * per_task + column, task_idx * EXPERTS + expert_idx] = 1.0
    for expert_idx in range(EXPERTS):
        table[TASKS * per_task + expert_idx, TASKS * EXPERTS + expert_idx] = 1.0
    return jnp.asarray(table, dtype=jnp.float32)


def gate_mix(rows, gate_weight):
    logits = jnp.dot(rows, gate_weight, preferred_element_type=jnp.float32)
    per_task = TASK_EXP + SHARED
    pieces = []
    for task_idx in range(TASKS):
        pieces.append(
            jax.nn.softmax(logits[:, task_idx * per_task : (task_idx + 1) * per_task], axis=-1)
        )
    pieces.append(jax.nn.softmax(logits[:, TASKS * per_task :], axis=-1))
    probs = jnp.concatenate(pieces, axis=1)
    mixed = jnp.dot(probs, routing_table(), precision=lax.Precision.HIGHEST)
    return mixed.reshape(rows.shape[0], TASKS + 1, EXPERTS)


def on_device(samples, gate_weight, up_weight, down_weight):
    local_experts = up_weight.shape[0]
    ex_count = lax.axis_size("ex")
    tp_count = lax.axis_size("tp")
    row_dev = samples.shape[0]
    width = samples.shape[1]
    piece = lax.all_gather(samples, ("ex", "tp"), axis=0, tiled=True)
    outputs = []
    for expert_idx in range(local_experts):
        outputs.append(
            jnp.maximum(
                jnp.dot(piece, up_weight[expert_idx], preferred_element_type=jnp.float32), 0.0
            ).astype(jnp.bfloat16)
        )
    hidden = jnp.stack(outputs, axis=1)
    partial_out = jnp.einsum(
        "rlf,lfd->rld", hidden, down_weight, preferred_element_type=jnp.float32
    )
    blocked = partial_out.reshape(ex_count, tp_count * row_dev, local_experts, width)
    summed = lax.psum_scatter(blocked, "tp", scatter_dimension=1, tiled=True)
    gathered = lax.all_to_all(summed, "ex", split_axis=0, concat_axis=2, tiled=True)[0]
    mixing = gate_mix(samples, gate_weight)
    result = jnp.einsum("rke,red->rkd", mixing, gathered, precision=lax.Precision.HIGHEST)
    return result.astype(jnp.bfloat16)


def solution(mesh):
    placed = (P(("ex", "tp"), None), P(), P("ex", None, "tp"), P("ex", "tp", None))
    return jax.shard_map(
        on_device,
        mesh=mesh,
        in_specs=placed,
        out_specs=P(("ex", "tp"), None, None),
        check_vma=False,
    )
```

profile of v0, /device:TPU:0, one launch (start us, length us, event | category | flops | bytes accessed | tf_op | source)
XLA Modules:
  0.0 185.9 jit_solution(10094937951658092538)
XLA Ops:
  6.5 78.9 %all-gather = bf16[32,6,2048]{2,1,0:T(8,128)(2,1)S(1)} all-gather(bf16[1,6,2048]{2,1,0:T(8,128)(2,1)} %bitcast.43), channel_id=1, replica_groups=mesh['ex'=8,'tp'=4] {'ex','tp'}, dimensions={0}, use_global_device_ids=true | all-gather | bytes 811008 | tf_op jit(solution)/shard_map/all_gather | solution.py:49
  85.5 0.3 reshape.20
  85.7 3.2 %fusion.21 = bf16[192,1,1024]{2,0,1:T(8,128)(2,1)S(1)} fusion(bf16[192,2048]{1,0:T(8,128)(2,1)S(1)} %reshape.20, bf16[2,2048,1024]{2,1,0:T(8,128)(2,1)} %param.7), kind=kOutput, calls=%fused_computation.12 | convolution fusion | flops 805699584 | bytes 5373952 | tf_op jit(solution)/shard_map/dot_general | solution.py:54
  88.9 3.2 %fusion.18 = bf16[192,1,1024]{2,0,1:T(8,128)(2,1)S(1)} fusion(bf16[192,2048]{1,0:T(8,128)(2,1)S(1)} %reshape.20, bf16[2,2048,1024]{2,1,0:T(8,128)(2,1)} %param.7), kind=kOutput, calls=%fused_computation.11 | convolution fusion | flops 805699584 | bytes 5373952 | tf_op jit(solution)/shard_map/dot_general | solution.py:54
  92.1 5.2 %fusion.24 = f32[2,192,2048]{2,1,0:T(8,128)S(1)} fusion(bf16[2,1024,2048]{2,1,0:T(8,128)(2,1)} %param.8, bf16[192,1,1024]{2,0,1:T(8,128)(2,1)S(1)} %fusion.21, bf16[192,1,1024]{2,0,1:T(8,128)(2,1)S(1)} %fusion.18), kind=kOutput, calls=%fused_computation.17 | convolution fusion | flops 1611005952 | bytes 12320768 | tf_op jit(solution)/shard_map/rlf,lfd->rld/dot_general | solution.py:58
  97.3 0.0 copy-start.1
  97.3 0.0 copy-start.5
  97.3 0.0 copy-start.6
  97.3 0.0 copy-start.4
  97.3 0.0 copy-start.3
  97.3 0.0 copy-start.2
  97.4 3.5 %copy.10 = f32[8,24,2,2048]{3,0,2,1:T(8,128)} copy(f32[8,24,2,2048]{3,1,0,2:T(8,128)S(1)} %bitcast.41) | data formatting | bytes 6291456 | tf_op jit(solution)/shard_map/reshape | solution.py:61
  100.8 0.0 reduce-scatter.2.cloned.1.call-update
  100.9 0.2 fusion.50
  101.0 0.2 slice_reduce_fusion
  101.2 0.2 slice_reduce_fusion.1
  101.5 0.2 fusion.37
  101.7 0.2 fusion.31
  101.9 0.2 convolution_add_fusion.3
  102.1 56.2 %reduce-scatter.2.cloned.1.call-done = f32[8,6,2,2048]{3,0,2,1:T(8,128)} async-done(((f32[8,24,2,2048]{3,0,2,1:T(8,128)}), f32[8,6,2,2048]{3,0,2,1:T(8,128)}) %reduce-scatter.2.cloned.1.call-update) | async-done | bytes 786448 | tf_op jit(solution)/shard_map/reduce_scatter | solution.py:62
  158.3 2.6 %copy.11 = f32[8,6,2,2048]{3,2,1,0:T(2,128)} copy(f32[8,6,2,2048]{3,0,2,1:T(8,128)} %reduce-scatter.2.cloned.1.call-done) | data formatting | bytes 1572864 | tf_op jit(solution)/shard_map/reduce_scatter | solution.py:62
  161.0 3.6 %all-to-all-start = ((f32[8,6,2,2048]{3,2,1,0:T(2,128)}), f32[8,6,2,2048]{3,2,1,0:T(2,128)S(1)}, u32[]{:S(2)}, u32[]{:S(2)}) async-start(f32[8,6,2,2048]{3,2,1,0:T(2,128)} %copy.11), calls=%async_computation.1 | async-start | bytes 1572864 | tf_op jit(solution)/shard_map/all_to_all | solution.py:63
  164.6 0.2 fusion.38
  164.8 0.2 convolution_add_fusion.2
  165.0 0.2 convolution_add_fusion.1
  165.2 0.2 convolution_add_fusion
  165.4 0.1 reshape.17
  165.5 11.7 %all-to-all-done = f32[8,6,2,2048]{3,2,1,0:T(2,128)S(1)} async-done(((f32[8,6,2,2048]{3,2,1,0:T(2,128)}), f32[8,6,2,2048]{3,2,1,0:T(2,128)S(1)}, u32[]{:S(2)}, u32[]{:S(2)}) %all-to-all-start) | async-done | bytes 786464 | tf_op jit(solution)/shard_map/all_to_all | solution.py:63
  177.2 0.1 copy.12
  177.2 0.5 squeeze.11
  177.8 0.5 convolution_convert_fusion
  178.3 0.8 copy.13
  (9 shorter events, 0.0 us)
Async XLA Ops:
  6.5 94.3 %copy-start = (bf16[2048,44]{0,1:T(8,128)(2,1)S(1)}, bf16[2048,44]{0,1:T(8,128)(2,1)}, u32[]{:S(2)}) copy-start(bf16[2048,44]{0,1:T(8,128)(2,1)} %param.6) | copy-start | bytes 540676
  6.5 151.8 %reduce-scatter.2.cloned.1.call-start = ((), (), s32[]{:S(2)}) async-start(), calls=%async_computation.2 | async-start | bytes 3932160 | tf_op jit(solution)/shard_map/reduce_scatter | solution.py:62
  97.3 3.6 %copy-start.1 = (bf16[6,2048]{1,0:T(8,128)(2,1)S(1)}, bf16[6,2048]{1,0:T(8,128)(2,1)}, u32[]{:S(2)}) copy-start(bf16[6,2048]{1,0:T(8,128)(2,1)} %param.5) | copy-start | bytes 73732
  97.3 4.4 %copy-start.5 = (f32[7,80]{1,0:T(8,128)S(1)}, f32[7,80]{1,0:T(8,128)}, u32[]{:S(2)}) copy-start(f32[7,80]{1,0:T(8,128)} %constant.12) | copy-start | bytes 6724
  97.3 4.6 %copy-start.6 = (f32[7,80]{1,0:T(8,128)S(1)}, f32[7,80]{1,0:T(8,128)}, u32[]{:S(2)}) copy-start(f32[7,80]{1,0:T(8,128)} %constant.13) | copy-start | bytes 6724
  97.3 67.5 %copy-start.4 = (f32[7,80]{1,0:T(8,128)S(1)}, f32[7,80]{1,0:T(8,128)}, u32[]{:S(2)}) copy-start(f32[7,80]{1,0:T(8,128)} %constant.14) | copy-start | bytes 6724
  97.3 67.7 %copy-start.3 = (f32[7,80]{1,0:T(8,128)S(1)}, f32[7,80]{1,0:T(8,128)}, u32[]{:S(2)}) copy-start(f32[7,80]{1,0:T(8,128)} %constant.15) | copy-start | bytes 6724
  97.3 67.9 %copy-start.2 = (f32[16,80]{1,0:T(8,128)S(1)}, f32[16,80]{1,0:T(8,128)}, u32[]{:S(2)}) copy-start(f32[16,80]{1,0:T(8,128)} %constant.16) | copy-start | bytes 15364
  161.0 16.2 %all-to-all-start = ((f32[8,6,2,2048]{3,2,1,0:T(2,128)}), f32[8,6,2,2048]{3,2,1,0:T(2,128)S(1)}, u32[]{:S(2)}, u32[]{:S(2)}) async-start(f32[8,6,2,2048]{3,2,1,0:T(2,128)} %copy.11), calls=%async_computation.1 | async-start | bytes 1572864 | tf_op jit(solution)/shard_map/all_to_all | solution.py:63
Sparse Core Ops, SparseCore 0:
  101.0 57.3 reduce-scatter.1
where the time goes:
time: 186 us
  blocking collectives  78.9 us (42%)
  waiting for transfers between devices  67.9 us (37%)
  between operations  13.5 us (7%)
  matrix products  13.2 us (7%)
  local copies, waits for them, and re-layouts  7.84 us (4%)
  starting transfers between devices  3.65 us (2%)
    all_gather x1, blocking collectives, on_device(): piece = lax.all_gather(samples, ('ex', 'tp'), axis=0, tiled=True)  78.9 us
    reduce_scatter x1, waiting for transfers between devices, on_device(): summed = lax.psum_scatter(blocked, 'tp', scatter_dimension=1, tiled=True)  56.2 us
    all_to_all x1, waiting for transfers between devices, on_device(): lax.all_to_all(summed, 'ex', split_axis=0, concat_axis=2, tiled=True)[0]  11.7 us
    dot_general x2, matrix products, on_device(): jnp.dot(piece, up_weight[expert_idx], preferred_element_type=jnp.float32)  6.35 us
    dot_general x1, matrix products, on_device(): jnp.einsum('rlf,lfd->rld', hidden, down_weight, preferred_element_type=jn...  5.18 us
  transfers between devices with their start and end apart: 2, of which 2 were waited for; matrix products, arithmetic and copies ran while one was open for 1% of the time, Pallas kernels for 0%

commit v1 on v0

--- a/solution.py
+++ b/solution.py
@@ -9,6 +9,18 @@
 SHARED = 4
 EXPERTS = 16
 GATES = 44
+
+
+def collect(x, axis, dim):
+    ways, here, turn = (lax.axis_size(axis), lax.axis_index(axis), x.shape[dim])
+    line, have = (x, 1)
+    while have < ways:
+        line = jnp.concatenate(
+            [line, lax.ppermute(line, axis, [(d, (d - have) % ways) for d in range(ways)])],
+            axis=dim,
+        )
+        have = 2 * have
+    return jnp.roll(line, here * turn, axis=dim)
 
 
 def routing_table():
@@ -46,7 +58,7 @@
     tp_count = lax.axis_size("tp")
     row_dev = samples.shape[0]
     width = samples.shape[1]
-    piece = lax.all_gather(samples, ("ex", "tp"), axis=0, tiled=True)
+    piece = collect(samples, ("ex", "tp"), 0)
     outputs = []
     for expert_idx in range(local_experts):
         outputs.append(

time: 186 us -> 154 us (0.83)
  blocking collectives: 78.9 us -> 0 us
  waiting for transfers between devices: 67.9 us -> 100 us
  starting transfers between devices: 3.65 us -> 11.7 us
  local copies, waits for them, and re-layouts: 7.84 us -> 11.3 us
  other arithmetic: 0.83 us -> 3.23 us
    all_gather x1 -> x0, blocking collectives: 78.9 us -> none  [on_device(): piece = lax.all_gather(samples, ('ex', 'tp'), axis=0, tiled=True)]
    ppermute x0 -> x5, waiting for transfers between devices: none -> 27.1 us  [collect(): lax.ppermute(line, axis, [(d, (d - have) % ways) for d in range(ways)])]
    ppermute x0 -> x5, starting transfers between devices: none -> 8.04 us  [collect(): lax.ppermute(line, axis, [(d, (d - have) % ways) for d in range(ways)])]
    reduce_scatter x1, waiting for transfers between devices: 56.2 us -> 61.5 us  [on_device(): summed = lax.psum_scatter(blocked, 'tp', scatter_dimension=1, tiled=True)]
    concatenate x0 -> x2, local copies, waits for them, and re-layouts: none -> 3.73 us  [the longest x1 2.57 us: collect(): return jnp.roll(line, here * turn, axis=dim)]
    concatenate x0 -> x3, other arithmetic: none -> 2.4 us  [collect(): jnp.concatenate([line, lax.ppermute(line, axis, [(d, (d - have) % ways) f...]
  transfers between devices with their start and end apart: 2 -> 7, of which waited for: 2 -> 7; matrix products, arithmetic and copies ran while one was open for 1% -> 1% of each run, Pallas kernels for 0% -> 0%
where the time goes in v1:
time: 154 us; the launch traced here: 153 us
  waiting for transfers between devices  100 us (65%)
  between operations  13.5 us (9%)
  matrix products  13.2 us (9%)
  starting transfers between devices  11.7 us (8%)
  local copies, waits for them, and re-layouts  11.3 us (7%)
  other arithmetic  3.23 us (2%)
    reduce_scatter x1, waiting for transfers between devices, on_device(): summed = lax.psum_scatter(blocked, 'tp', scatter_dimension=1, tiled=True)  61.5 us
    ppermute x5, waiting for transfers between devices, collect(): lax.ppermute(line, axis, [(d, (d - have) % ways) for d in range(ways)])  27.1 us
    all_to_all x1, waiting for transfers between devices, on_device(): lax.all_to_all(summed, 'ex', split_axis=0, concat_axis=2, tiled=True)[0]  11.7 us
    ppermute x5, starting transfers between devices, collect(): lax.ppermute(line, axis, [(d, (d - have) % ways) for d in range(ways)])  8.04 us
    dot_general x2, matrix products, on_device(): jnp.dot(piece, up_weight[expert_idx], preferred_element_type=jnp.float32)  6.36 us
    dot_general x1, matrix products, on_device(): jnp.einsum('rlf,lfd->rld', hidden, down_weight, preferred_element_type=jn...  5.18 us
    all_to_all x1, starting transfers between devices, on_device(): lax.all_to_all(summed, 'ex', split_axis=0, concat_axis=2, tiled=True)[0]  3.66 us
    reshape x1, local copies, waits for them, and re-layouts, on_device(): partial_out.reshape(ex_count, tp_count * row_dev, local_experts, width)  3.49 us
  transfers between devices with their start and end apart: 7, of which 7 were waited for; matrix products, arithmetic and copies ran while one was open for 1% of the time, Pallas kernels for 0%

profile of v1, /device:TPU:0, one launch (start us, length us, event | category | flops | bytes accessed | tf_op | source)
XLA Modules:
  0.0 153.3 jit_solution(12092282936366268955)
XLA Ops:
  6.5 6.4 %collective-permute-start = (bf16[6,2048]{1,0:T(8,128)(2,1)}, bf16[6,2048]{1,0:T(8,128)(2,1)S(1)}, u32[]{:S(2)}, u32[]{:S(2)}) collective-permute-start(bf16[6,2048]{1,0:T(8,128)(2,1)} %param.5), channel_id=1, source_target_pairs={{0,31},{1,0},{2,1},{3,2},{4,3},{5,4},{6,5},{7,6},{8,7},{9,8},{10,9... | collective-permute-start | bytes 73736 | tf_op jit(solution)/shard_map/ppermute | solution.py:19
  12.9 1.9 %collective-permute-done = bf16[6,2048]{1,0:T(8,128)(2,1)S(1)} collective-permute-done((bf16[6,2048]{1,0:T(8,128)(2,1)}, bf16[6,2048]{1,0:T(8,128)(2,1)S(1)}, u32[]{:S(2)}, u32[]{:S(2)}) %collective-permute-start) | collective-permute-done | bytes 24608 | tf_op jit(solution)/shard_map/ppermute | solution.py:19
  14.9 0.8 pad_maximum_fusion.2
  15.7 5.7 %collective-permute-done.1 = bf16[12,2048]{1,0:T(8,128)(2,1)S(1)} collective-permute-done((bf16[12,2048]{1,0:T(8,128)(2,1)S(1)}, bf16[12,2048]{1,0:T(8,128)(2,1)S(1)}, u32[]{:S(2)}, u32[]{:S(2)}) %collective-permute-start.1) | collective-permute-done | bytes 49184 | tf_op jit(solution)/shard_map/ppermute | solution.py:19
  21.5 0.8 pad_maximum_fusion.1
  22.3 2.2 %collective-permute-done.2 = bf16[24,2048]{1,0:T(8,128)(2,1)S(1)} collective-permute-done((bf16[24,2048]{1,0:T(8,128)(2,1)S(1)}, bf16[24,2048]{1,0:T(8,128)(2,1)S(1)}, u32[]{:S(2)}, u32[]{:S(2)}) %collective-permute-start.2) | collective-permute-done | bytes 98336 | tf_op jit(solution)/shard_map/ppermute | solution.py:19
  24.5 0.8 pad_maximum_fusion
  25.5 7.4 %collective-permute-done.3 = bf16[48,2048]{1,0:T(8,128)(2,1)S(1)} collective-permute-done((bf16[48,2048]{1,0:T(8,128)(2,1)S(1)}, bf16[48,2048]{1,0:T(8,128)(2,1)S(1)}, u32[]{:S(2)}, u32[]{:S(2)}) %collective-permute-start.3) | collective-permute-done | bytes 196640 | tf_op jit(solution)/shard_map/ppermute | solution.py:19
  32.9 1.2 concatenate.29
  34.1 1.3 collective-permute-start.4
  35.4 9.9 %collective-permute-done.4 = bf16[96,2048]{1,0:T(8,128)(2,1)S(1)} collective-permute-done((bf16[96,2048]{1,0:T(8,128)(2,1)S(1)}, bf16[96,2048]{1,0:T(8,128)(2,1)S(1)}, u32[]{:S(2)}, u32[]{:S(2)}) %collective-permute-start.4) | collective-permute-done | bytes 393248 | tf_op jit(solution)/shard_map/ppermute | solution.py:19
  45.3 2.6 %concatenate.30 = bf16[384,2048]{1,0:T(8,128)(2,1)S(1)} concatenate(bf16[6,2048]{1,0:T(8,128)(2,1)} %param.5, bf16[6,2048]{1,0:T(8,128)(2,1)S(1)} %collective-permute-done, bf16[12,2048]{1,0:T(8,128)(2,1)S(1)} %collective-permute-done.1, bf16[24,2048]{1,0:T(8,128)(2,1)S(1)} %collective-permute-done.2, bf16[48,2048]{1,0:T(8,128)(2,1)S(1)} %collective-permute-done.3, ...), dimensions={0} | concatenate | bytes 3145728 | tf_op jit(solution)/shard_map/jit(_roll_dynamic)/concatenate | solution.py:23
  47.9 3.2 %fusion.18 = bf16[192,1,1024]{2,0,1:T(8,128)(2,1)S(1)} fusion(bf16[2,2048,1024]{2,1,0:T(8,128)(2,1)} %param.7, bf16[384,2048]{1,0:T(8,128)(2,1)S(1)} %concatenate.30, s32[]{:T(128)S(6)} %select_n.14), kind=kOutput, calls=%fused_computation.11 | convolution fusion | flops 805699584 | bytes 5373956 | tf_op jit(solution)/shard_map/dot_general | solution.py:66
  51.0 3.2 %fusion.21 = bf16[192,1,1024]{2,0,1:T(8,128)(2,1)S(1)} fusion(bf16[2,2048,1024]{2,1,0:T(8,128)(2,1)} %param.7, bf16[384,2048]{1,0:T(8,128)(2,1)S(1)} %concatenate.30, s32[]{:T(128)S(6)} %select_n.14), kind=kOutput, calls=%fused_computation.12 | convolution fusion | flops 805699584 | bytes 5373956 | tf_op jit(solution)/shard_map/dot_general | solution.py:66
  54.2 5.2 %fusion.24 = f32[2,192,2048]{2,1,0:T(8,128)S(1)} fusion(bf16[2,1024,2048]{2,1,0:T(8,128)(2,1)} %param.8, bf16[192,1,1024]{2,0,1:T(8,128)(2,1)S(1)} %fusion.21, bf16[192,1,1024]{2,0,1:T(8,128)(2,1)S(1)} %fusion.18), kind=kOutput, calls=%fused_computation.17 | convolution fusion | flops 1611005952 | bytes 12320768 | tf_op jit(solution)/shard_map/rlf,lfd->rld/dot_general | solution.py:70
  59.5 3.5 %copy.10 = f32[8,24,2,2048]{3,0,2,1:T(8,128)} copy(f32[8,24,2,2048]{3,1,0,2:T(8,128)S(1)} %bitcast.38) | data formatting | bytes 6291456 | tf_op jit(solution)/shard_map/reshape | solution.py:73
  63.2 0.2 slice_reduce_fusion
  63.4 0.2 slice_reduce_fusion.1
  63.6 0.2 fusion.39
  63.8 0.2 fusion.33
  64.0 0.2 convolution_add_fusion.3
  64.2 61.5 %reduce-scatter.2.cloned.1.call-done = f32[8,6,2,2048]{3,0,2,1:T(8,128)} async-done(((f32[8,24,2,2048]{3,0,2,1:T(8,128)}), f32[8,6,2,2048]{3,0,2,1:T(8,128)}) %reduce-scatter.2.cloned.1.call-update) | async-done | bytes 786448 | tf_op jit(solution)/shard_map/reduce_scatter | solution.py:74
  125.7 2.6 %copy.11 = f32[8,6,2,2048]{3,2,1,0:T(2,128)} copy(f32[8,6,2,2048]{3,0,2,1:T(8,128)} %reduce-scatter.2.cloned.1.call-done) | data formatting | bytes 1572864 | tf_op jit(solution)/shard_map/reduce_scatter | solution.py:74
  128.3 3.7 %all-to-all-start = ((f32[8,6,2,2048]{3,2,1,0:T(2,128)}), f32[8,6,2,2048]{3,2,1,0:T(2,128)S(1)}, u32[]{:S(2)}, u32[]{:S(2)}) async-start(f32[8,6,2,2048]{3,2,1,0:T(2,128)} %copy.11), calls=%async_computation.1 | async-start | bytes 1572864 | tf_op jit(solution)/shard_map/all_to_all | solution.py:75
  132.0 0.2 fusion.40
  132.2 0.2 convolution_add_fusion.2
  132.4 0.2 convolution_add_fusion.1
  132.6 0.2 convolution_add_fusion
  132.9 11.7 %all-to-all-done = f32[8,6,2,2048]{3,2,1,0:T(2,128)S(1)} async-done(((f32[8,6,2,2048]{3,2,1,0:T(2,128)}), f32[8,6,2,2048]{3,2,1,0:T(2,128)S(1)}, u32[]{:S(2)}, u32[]{:S(2)}) %all-to-all-start) | async-done | bytes 786464 | tf_op jit(solution)/shard_map/all_to_all | solution.py:75
  144.6 0.5 squeeze.11
  145.1 0.5 convolution_convert_fusion
  145.7 0.8 copy.13
  (22 shorter events, 0.7 us)
Async XLA Ops:
  6.5 56.4 %copy-start = (bf16[2048,44]{0,1:T(8,128)(2,1)S(1)}, bf16[2048,44]{0,1:T(8,128)(2,1)}, u32[]{:S(2)}) copy-start(bf16[2048,44]{0,1:T(8,128)(2,1)} %param.6) | copy-start | bytes 540676
  6.5 119.2 %reduce-scatter.2.cloned.1.call-start = ((), (), s32[]{:S(2)}) async-start(), calls=%async_computation.2 | async-start | bytes 3932160 | tf_op jit(solution)/shard_map/reduce_scatter | solution.py:74
  6.5 8.3 %collective-permute-start = (bf16[6,2048]{1,0:T(8,128)(2,1)}, bf16[6,2048]{1,0:T(8,128)(2,1)S(1)}, u32[]{:S(2)}, u32[]{:S(2)}) collective-permute-start(bf16[6,2048]{1,0:T(8,128)(2,1)} %param.5), channel_id=1, source_target_pairs={{0,31},{1,0},{2,1},{3,2},{4,3},{5,4},{6,5},{7,6},{8,7},{9,8},{10,9... | collective-permute-start | bytes 73736 | tf_op jit(solution)/shard_map/ppermute | solution.py:19
  15.6 5.8 %collective-permute-start.1 = (bf16[12,2048]{1,0:T(8,128)(2,1)S(1)}, bf16[12,2048]{1,0:T(8,128)(2,1)S(1)}, u32[]{:S(2)}, u32[]{:S(2)}) collective-permute-start(bf16[12,2048]{1,0:T(8,128)(2,1)S(1)} %pad_maximum_fusion.2), channel_id=1, source_target_pairs={{0,30},{1,31},{2,0},{3,1},{4,2},{5,3},{6,4},{7,5},{8,6},{9,7},{10,... | collective-permute-start | bytes 147464 | tf_op jit(solution)/shard_map/ppermute | solution.py:19
  22.3 2.3 %collective-permute-start.2 = (bf16[24,2048]{1,0:T(8,128)(2,1)S(1)}, bf16[24,2048]{1,0:T(8,128)(2,1)S(1)}, u32[]{:S(2)}, u32[]{:S(2)}) collective-permute-start(bf16[24,2048]{1,0:T(8,128)(2,1)S(1)} %pad_maximum_fusion.1), channel_id=1, source_target_pairs={{0,28},{1,29},{2,30},{3,31},{4,0},{5,1},{6,2},{7,3},{8,4},{9,5},{1... | collective-permute-start | bytes 294920 | tf_op jit(solution)/shard_map/ppermute | solution.py:19
  25.4 7.6 %collective-permute-start.3 = (bf16[48,2048]{1,0:T(8,128)(2,1)S(1)}, bf16[48,2048]{1,0:T(8,128)(2,1)S(1)}, u32[]{:S(2)}, u32[]{:S(2)}) collective-permute-start(bf16[48,2048]{1,0:T(8,128)(2,1)S(1)} %pad_maximum_fusion), channel_id=1, source_target_pairs={{0,24},{1,25},{2,26},{3,27},{4,28},{5,29},{6,30},{7,31},{8,0},{9,1... | collective-permute-start | bytes 589832 | tf_op jit(solution)/shard_map/ppermute | solution.py:19
  34.1 11.2 %collective-permute-start.4 = (bf16[96,2048]{1,0:T(8,128)(2,1)S(1)}, bf16[96,2048]{1,0:T(8,128)(2,1)S(1)}, u32[]{:S(2)}, u32[]{:S(2)}) collective-permute-start(bf16[96,2048]{1,0:T(8,128)(2,1)S(1)} %concatenate.29), channel_id=1, source_target_pairs={{0,16},{1,17},{2,18},{3,19},{4,20},{5,21},{6,22},{7,23},{8,24},{9,... | collective-permute-start | bytes 1179656 | tf_op jit(solution)/shard_map/ppermute | solution.py:19
  59.4 3.6 %copy-start.1 = (bf16[6,2048]{1,0:T(8,128)(2,1)S(1)}, bf16[6,2048]{1,0:T(8,128)(2,1)}, u32[]{:S(2)}) copy-start(bf16[6,2048]{1,0:T(8,128)(2,1)} %param.5) | copy-start | bytes 73732
  59.4 4.4 %copy-start.6 = (f32[7,80]{1,0:T(8,128)S(1)}, f32[7,80]{1,0:T(8,128)}, u32[]{:S(2)}) copy-start(f32[7,80]{1,0:T(8,128)} %constant.44) | copy-start | bytes 6724
  59.4 4.6 %copy-start.5 = (f32[7,80]{1,0:T(8,128)S(1)}, f32[7,80]{1,0:T(8,128)}, u32[]{:S(2)}) copy-start(f32[7,80]{1,0:T(8,128)} %constant.45) | copy-start | bytes 6724
  62.9 69.2 %copy-start.4 = (f32[7,80]{1,0:T(8,128)S(1)}, f32[7,80]{1,0:T(8,128)}, u32[]{:S(2)}) copy-start(f32[7,80]{1,0:T(8,128)} %constant.46) | copy-start | bytes 6724
  63.0 69.4 %copy-start.3 = (f32[7,80]{1,0:T(8,128)S(1)}, f32[7,80]{1,0:T(8,128)}, u32[]{:S(2)}) copy-start(f32[7,80]{1,0:T(8,128)} %constant.47) | copy-start | bytes 6724
  63.0 69.6 %copy-start.2 = (f32[16,80]{1,0:T(8,128)S(1)}, f32[16,80]{1,0:T(8,128)}, u32[]{:S(2)}) copy-start(f32[16,80]{1,0:T(8,128)} %constant.48) | copy-start | bytes 15364
  128.3 16.2 %all-to-all-start = ((f32[8,6,2,2048]{3,2,1,0:T(2,128)}), f32[8,6,2,2048]{3,2,1,0:T(2,128)S(1)}, u32[]{:S(2)}, u32[]{:S(2)}) async-start(f32[8,6,2,2048]{3,2,1,0:T(2,128)} %copy.11), calls=%async_computation.1 | async-start | bytes 1572864 | tf_op jit(solution)/shard_map/all_to_all | solution.py:75
Sparse Core Ops, SparseCore 0:
  63.1 62.5 reduce-scatter.1
